TPU v7x, 128 devices: a whole 4x4x4 slice. The times are simulated.
128 devices in a mesh: gx: 4 (over x), gz: 4 (over y_lo, core), ta: 8 (over z, y_hi).
Axes of the slice: x: 4, y: 4 (y_hi: 2, y_lo: 2; y = y_hi * 2 + y_lo), z: 4, core: 2. Of those that a mesh axis runs over, the one named last changes fastest.
Arguments:
- propagator: float32 [2, 12, 12, 1048576], P(None, None, None, ('gx', 'gz', 'ta')), may hold values from -6 to 6
- momenta: int32 [512, 4], P(('gx', 'gz', 'ta')), may hold values from -16 to 15
- gamma_index: int32 [16], replicated, may hold values from 0 to 15, each once
Outputs:
- vertices: float32 [512, 16, 2, 12, 12], P(('gx', 'gz', 'ta'))
Inputs may be any that keep to these rules, and one draw needn't show every extreme that they name: `momenta`: A momentum component enters only modulo the lattice length along its direction. `gamma_index`: every mask of 0 to 15 appears once.
All inputs are finite; a program needn't handle non-finite values.
Results may differ from a plain program's by a relative error of at most 0.0001.
Values sent between devices are 32-bit elements; how exact they have to be, the bound alone decides.
A program may use at most 128 MiB of HBM per device.

v0:
```python
import math
import jax
import jax.numpy as jnp
import numpy as np
from jax import lax
from jax.sharding import PartitionSpec as P

LX = 32
LY = 32
LZ = 32
LT = 32


def in_blocks(array, dim, devices):
    before, after = (array.shape[:dim], array.shape[dim + 1 :])
    return jnp.moveaxis(array.reshape(*before, devices, -1, *after), dim, 0)


def summed_on_arrival(array, axis, dim):
    devices = lax.axis_size(axis)
    blocks = lax.all_to_all(in_blocks(array, dim, devices), axis, 0, 0, tiled=True)
    return jnp.sum(blocks, axis=0)


def clifford_table():
    zeros = np.zeros((4, 4))
    first = (zeros, np.array([[0, 0, 0, 1], [0, 0, 1, 0], [0, -1, 0, 0], [-1, 0, 0, 0]]))
    second = (np.array([[0, 0, 0, -1], [0, 0, 1, 0], [0, 1, 0, 0], [-1, 0, 0, 0]]), zeros)
    third = (zeros, np.array([[0, 0, 1, 0], [0, 0, 0, -1], [-1, 0, 0, 0], [0, 1, 0, 0]]))
    fourth = (np.array([[0, 0, 1, 0], [0, 0, 0, 1], [1, 0, 0, 0], [0, 1, 0, 0]]), zeros)
    basis = [first, second, third, fourth]
    tables_re = []
    tables_im = []
    for mask in range(16):
        matrix_re = np.identity(4)
        matrix_im = np.zeros((4, 4))
        for bit in range(4):
            if mask >> bit & 1:
                basis_re, basis_im = basis[bit]
                new_re = matrix_re @ basis_re - matrix_im @ basis_im
                new_im = matrix_re @ basis_im + matrix_im @ basis_re
                matrix_re, matrix_im = (new_re, new_im)
        tables_re.append(matrix_re)
        tables_im.append(matrix_im)
    return (np.stack(tables_re), np.stack(tables_im))


def select_gammas(gamma_index):
    table_re, table_im = clifford_table()
    onehot = (gamma_index[:, None] == jnp.arange(16, dtype=jnp.int32)[None, :]).astype(jnp.float32)
    high = lax.Precision.HIGHEST
    chosen_re = jnp.einsum(
        "gk,kst->gst", onehot, jnp.asarray(table_re, jnp.float32), precision=high
    )
    chosen_im = jnp.einsum(
        "gk,kst->gst", onehot, jnp.asarray(table_im, jnp.float32), precision=high
    )
    return (chosen_re, chosen_im)


def vertices_of(spec_re, spec_im, gamma_re, gamma_im):
    high = lax.Precision.HIGHEST
    count = spec_re.shape[0]
    split_re = spec_re.reshape(count, 4, 3, 12)
    split_im = spec_im.reshape(count, 4, 3, 12)
    turned_re = (
        jnp.einsum("gst,mtcb->mgscb", gamma_re, split_re, precision=high)
        - jnp.einsum("gst,mtcb->mgscb", gamma_im, split_im, precision=high)
    ).reshape(count, 16, 12, 12)
    turned_im = (
        jnp.einsum("gst,mtcb->mgscb", gamma_re, split_im, precision=high)
        + jnp.einsum("gst,mtcb->mgscb", gamma_im, split_re, precision=high)
    ).reshape(count, 16, 12, 12)
    result_re = jnp.einsum("mka,mgkb->mgab", spec_re, turned_re, precision=high) + jnp.einsum(
        "mka,mgkb->mgab", spec_im, turned_im, precision=high
    )
    result_im = jnp.einsum("mka,mgkb->mgab", spec_re, turned_im, precision=high) - jnp.einsum(
        "mka,mgkb->mgab", spec_im, turned_re, precision=high
    )
    return jnp.stack([result_re, result_im], axis=2)


def site_coordinates(local_sites):
    block_x = LX // lax.axis_size("gx")
    block_z = LZ // lax.axis_size("gz")
    block_t = LT // lax.axis_size("ta")
    linear = jnp.arange(local_sites, dtype=jnp.int32)
    coord_t = linear % block_t + lax.axis_index("ta") * block_t
    coord_z = linear // block_t % block_z + lax.axis_index("gz") * block_z
    coord_y = linear // (block_t * block_z) % LY
    coord_x = linear // (block_t * block_z * LY) + lax.axis_index("gx") * block_x
    return jnp.stack([coord_x, coord_y, coord_z, coord_t])


def make_term(momentum_rows, coords, plain_re, diff_part, summed_part):
    lengths = (LX, LY, LZ, LT)
    common = lengths[0]
    for length in lengths[1:]:
        common = common * length // math.gcd(common, length)
    high = lax.Precision.HIGHEST

    def single_block(waves):
        phase_index = jnp.zeros((waves.shape[0], coords.shape[1]), jnp.int32)
        for direction in range(4):
            reduced = waves[:, direction] % lengths[direction] * (common // lengths[direction])
            phase_index = phase_index + reduced[:, None] * coords[direction][None, :]
        phase_index = phase_index % common
        angle = phase_index.astype(jnp.float32) * (2.0 * math.pi / float(common))
        cosine = jnp.cos(angle)
        sine = jnp.sin(angle)
        first = jnp.einsum("ms,cs->mc", cosine - sine, plain_re, precision=high)
        second = jnp.einsum("ms,cs->mc", cosine, diff_part, precision=high)
        third = jnp.einsum("ms,cs->mc", -sine, summed_part, precision=high)
        return jnp.concatenate([first - third, first + second], axis=1)

    def term(start, count):
        width = math.gcd(count, 512)
        picked = momentum_rows
        picked = picked.reshape(count // width, width, 4)
        return lax.map(single_block, picked).reshape(count, 288)

    return term


def body(propagator, momenta, gamma_index):
    local_sites = propagator.shape[3]
    mine = momenta.shape[0]
    coords = site_coordinates(local_sites)
    plain_re = propagator[0].reshape(144, local_sites)
    plain_im = propagator[1].reshape(144, local_sites)
    diff_part = plain_im - plain_re
    summed_part = plain_re + plain_im
    gathered = lax.all_gather(momenta, ("gx", "gz", "ta"), axis=0, tiled=True)
    spatial = lax.axis_size("gx") * lax.axis_size("gz")
    ordered = gathered.reshape(spatial, lax.axis_size("ta"), mine, 4)
    ordered = jnp.transpose(ordered, (1, 0, 2, 3)).reshape(-1, 4)
    term = make_term(ordered, coords, plain_re, diff_part, summed_part)
    partial_value = summed_on_arrival(
        term(jnp.int32(0), spatial * mine * lax.axis_size("ta")), "ta", 0
    )
    spectrum = summed_on_arrival(partial_value, ("gx", "gz"), 0)
    spectrum = spectrum * (1.0 / math.sqrt(float(LX * LY * LZ * LT)))
    spectrum = spectrum.reshape(mine, 2, 12, 12)
    gamma_re, gamma_im = select_gammas(gamma_index)
    return vertices_of(spectrum[:, 0], spectrum[:, 1], gamma_re, gamma_im)


def solution(mesh):
    placed = (P(None, None, None, ("gx", "gz", "ta")), P(("gx", "gz", "ta"), None), P())
    return jax.shard_map(
        body,
        mesh=mesh,
        in_specs=placed,
        out_specs=P(("gx", "gz", "ta"), None, None, None, None),
        check_vma=False,
    )
```

profile of v0, /device:TPU:1, one launch (start us, length us, event | category | flops | bytes accessed | tf_op | source)
XLA Modules:
  0.0 679.2 jit_solution(13706072542922024557)
XLA Ops:
  0.0 32.7 %slice_reduce_fusion = (f32[12,12,8192]{2,1,0:T(8,128)}, f32[12,12,8192]{2,1,0:T(8,128)}) fusion(f32[2,12,12,8192]{3,0,2,1:T(2,128)} %param.5), kind=kLoop, calls=%fused_computation.15 | loop fusion | bytes 18874368 | tf_op jit(solution)/shard_map/slice | solution.py:130
  32.7 6.0 reshape_squeeze.12
  38.7 6.0 reshape_squeeze.13
  44.7 6.9 %fusion.108 = f32[144,8192]{1,0:T(8,128)} fusion(f32[144,8192]{1,0:T(8,128)} %reshape_squeeze.13, f32[144,8192]{1,0:T(8,128)} %reshape_squeeze.12), kind=kLoop, calls=%fused_computation.13.clone.clone.clone.2 | loop fusion | flops 1179648 | bytes 14155776 | tf_op jit(solution)/shard_map/while/body/eval_jaxpr/ms,cs->mc/dot_general | solution.py:112
  51.6 0.0 slice-done
  51.6 0.0 slice-done.1
  51.6 1.2 copy-done
  52.8 3.0 fusion.110
  55.8 0.0 copy-done.1
  55.8 310.6 %all-gather = s32[128,4,4]{2,1,0:T(4,128)S(1)} all-gather(s32[1,4,4]{2,1,0:T(4,128)S(1)} %bitcast.115), channel_id=1, replica_groups=mesh['gx'=4,'gz'=4,'ta'=8] {'gx','gz','ta'}, dimensions={0}, use_global_device_ids=true | all-gather | bytes 8256 | tf_op jit(solution)/shard_map/all_gather | solution.py:133
  366.4 1.0 copy.58
  367.4 0.2 squeeze.19
  367.7 0.0 slice-start.3
  367.7 0.0 slice-start.6
  367.7 72.3 %fusion.106 = f32[512,8192]{1,0:T(8,128)} fusion(s32[8192]{0:T(1024)S(1)} %get-tuple-element.46, s32[512]{0:T(512)S(1)} %bitcast.106, s32[8192]{0:T(1024)S(1)} %get-tuple-element.45, s32[512]{0:T(512)S(1)} %bitcast.109, s32[8192]{0:T(1024)S(1)} %get-tuple-element.42, s32[512]{0:T(512)S(1)} %bitcast.112, s32[8192]{0:T(1024)S(1)} %get-tuple-element.44, ...), kind=kLoop, calls=%fused_computation.9.clone.1 | loop fusion | flops 88080384 | bytes 16916480 | tf_op jit(solution)/shard_map/while/body/eval_jaxpr/ms,cs->mc/dot_general | solution.py:111
  440.0 0.0 slice-done.2
  440.0 0.0 slice-start.7
  440.0 0.0 slice-start.4
  440.0 20.4 %fusion.5 = f32[512,144]{0,1:T(8,128)S(1)} fusion(f32[144,8192]{1,0:T(8,128)S(1)} %bitcast.86, f32[512,8192]{1,0:T(8,128)} %fusion.106), kind=kOutput, calls=%fused_computation.8 | convolution fusion | flops 7247757312 | bytes 21790720 | tf_op jit(solution)/shard_map/while/body/eval_jaxpr/ms,cs->mc/dot_general | solution.py:111
  460.5 0.0 slice-start.5
  460.5 80.0 %fusion.20 = f32[512,144]{0,1:T(8,128)S(1)} fusion(f32[512,144]{0,1:T(8,128)S(1)} %fusion.5, s32[8192]{0:T(1024)S(1)} %get-tuple-element.46, s32[512]{0:T(512)S(1)} %bitcast.107, s32[8192]{0:T(1024)S(1)} %get-tuple-element.45, s32[512]{0:T(512)S(1)} %bitcast.110, s32[8192]{0:T(1024)S(1)} %get-tuple-element.42, s32[512]{0:T(512)S(1)} %bitcast.113, ...), kind=kOutput, calls=%fused_computation.25 | convolution fusion | flops 7331717120 | bytes 5447680 | tf_op jit(solution)/shard_map/while/body/eval_jaxpr/ms,cs->mc/dot_general | solution.py:112
  540.5 0.0 copy-start.2
  540.5 0.0 copy-start.4
  540.6 0.0 copy-start.3
  540.6 94.9 %fusion.25 = f32[512,144]{0,1:T(8,128)S(1)} fusion(f32[512,144]{0,1:T(8,128)S(1)} %fusion.5, s32[8192]{0:T(1024)S(1)} %get-tuple-element.46, s32[512]{0:T(512)S(1)} %bitcast.108, s32[8192]{0:T(1024)S(1)} %get-tuple-element.45, s32[512]{0:T(512)S(1)} %bitcast.111, s32[8192]{0:T(1024)S(1)} %get-tuple-element.42, s32[512]{0:T(512)S(1)} %bitcast.114, ...), kind=kOutput, calls=%fused_computation.26 | convolution fusion | flops 7335911424 | bytes 5447680 | tf_op jit(solution)/shard_map/while/body/eval_jaxpr/ms,cs->mc/dot_general | solution.py:113
  635.5 1.2 copy.59
  636.7 3.5 all-to-all-start
  640.2 0.2 fusion.61
  640.4 10.2 %all-to-all-done = f32[8,64,288]{2,1,0:T(8,128)S(1)} async-done(((f32[8,64,288]{2,1,0:T(8,128)}), f32[8,64,288]{2,1,0:T(8,128)S(1)}, u32[]{:S(2)}, u32[]{:S(2)}) %all-to-all-start) | async-done | bytes 589856 | tf_op jit(solution)/shard_map/all_to_all | solution.py:21
  650.6 0.7 reshape.89
  651.3 14.7 %all-to-all-start.1 = ((f32[16,4,288]{2,1,0:T(4,128)}), f32[16,4,288]{2,1,0:T(4,128)S(1)}, u32[]{:S(2)}, u32[]{:S(2)}) async-start(f32[16,4,288]{2,1,0:T(4,128)} %reshape.89), calls=%async_computation.1 | async-start | bytes 196608 | tf_op jit(solution)/shard_map/all_to_all | solution.py:21
  666.0 0.2 fusion.60
  666.2 5.8 all-to-all-done.1
  672.0 0.1 mul.133
  672.2 0.6 fusion.54
  672.7 0.6 fusion.58
  673.3 0.6 fusion.18
  673.9 0.2 copy.71
  674.1 0.4 copy.72
  674.4 0.5 fusion.46
  674.9 0.6 fusion.19
  675.5 0.2 copy.67
  675.7 0.4 copy.68
  676.0 0.5 fusion.48
  676.5 0.5 fusion.16
  677.0 0.5 fusion.17
  677.4 0.1 pad_maximum_fusion
  677.5 1.5 copy.75
  (27 shorter events, 0.2 us)
Async XLA Ops:
  38.7 12.9 %slice-start = ((s8[4718592]{0:T(1024)(128)(4,1)}), s8[524288]{0:T(1024)(128)(4,1)S(1)}, s32[]{:S(2)}) async-start(s8[4718592]{0:T(1024)(128)(4,1)} %bitcast.83), calls=%async_computation.2 | async-start | bytes 1048576
  44.7 6.9 %slice-start.1 = ((s8[4718592]{0:T(1024)(128)(4,1)}), s8[4194304]{0:T(1024)(128)(4,1)S(1)}, s32[]{:S(2)}) async-start(s8[4718592]{0:T(1024)(128)(4,1)} %bitcast.83), calls=%async_computation.3 | async-start | bytes 8388608
  44.7 8.1 %copy-start = (f32[144,8192]{1,0:T(8,128)S(1)}, f32[144,8192]{1,0:T(8,128)}, u32[]{:S(2)}) copy-start(f32[144,8192]{1,0:T(8,128)} %reshape_squeeze.13) | copy-start | bytes 14155780
  44.7 11.1 %copy-start.1 = (s32[4,4]{1,0:T(4,128)S(1)}, s32[4,4]{1,0:T(4,128)}, u32[]{:S(2)}) copy-start(s32[4,4]{1,0:T(4,128)} %param.6) | copy-start | bytes 196
  52.8 387.2 %slice-start.2 = ((s8[4718592]{0:T(1024)(128)(4,1)}), s8[524288]{0:T(1024)(128)(4,1)S(1)}, s32[]{:S(2)}) async-start(s8[4718592]{0:T(1024)(128)(4,1)} %bitcast.85), calls=%async_computation.4 | async-start | bytes 1048576
  367.7 72.3 %slice-start.3 = ((s8[4718592]{0:T(1024)(128)(4,1)}), s8[4194304]{0:T(1024)(128)(4,1)S(1)}, s32[]{:S(2)}) async-start(s8[4718592]{0:T(1024)(128)(4,1)} %bitcast.85), calls=%async_computation.5 | async-start | bytes 8388608
  367.7 92.8 %slice-start.6 = ((s8[4718592]{0:T(1024)(128)(4,1)}), s8[4194304]{0:T(1024)(128)(4,1)S(1)}, s32[]{:S(2)}) async-start(s8[4718592]{0:T(1024)(128)(4,1)} %bitcast.89), calls=%async_computation.8 | async-start | bytes 8388608
  440.0 20.5 %slice-start.7 = ((s8[4718592]{0:T(1024)(128)(4,1)}), s8[524288]{0:T(1024)(128)(4,1)S(1)}, s32[]{:S(2)}) async-start(s8[4718592]{0:T(1024)(128)(4,1)} %bitcast.89), calls=%async_computation.9 | async-start | bytes 1048576
  440.0 100.5 %slice-start.4 = ((s8[4718592]{0:T(1024)(128)(4,1)}), s8[524288]{0:T(1024)(128)(4,1)S(1)}, s32[]{:S(2)}) async-start(s8[4718592]{0:T(1024)(128)(4,1)} %bitcast.87), calls=%async_computation.6 | async-start | bytes 1048576
  460.5 80.0 %slice-start.5 = ((s8[4718592]{0:T(1024)(128)(4,1)}), s8[4194304]{0:T(1024)(128)(4,1)S(1)}, s32[]{:S(2)}) async-start(s8[4718592]{0:T(1024)(128)(4,1)} %bitcast.87), calls=%async_computation.7 | async-start | bytes 8388608
  540.5 99.7 %copy-start.2 = (s32[16]{0:T(128)S(1)}, s32[16]{0:T(128)}, u32[]{:S(2)}) copy-start(s32[16]{0:T(128)} %param.7) | copy-start | bytes 196
  540.5 99.7 %copy-start.4 = (f32[16,16]{0,1:T(8,128)S(1)}, f32[16,16]{0,1:T(8,128)}, u32[]{:S(2)}) copy-start(f32[16,16]{0,1:T(8,128)} %constant.146) | copy-start | bytes 3076
  540.6 125.4 %copy-start.3 = (f32[16,16]{0,1:T(8,128)S(1)}, f32[16,16]{0,1:T(8,128)}, u32[]{:S(2)}) copy-start(f32[16,16]{0,1:T(8,128)} %constant.147) | copy-start | bytes 3076
  636.7 13.9 %all-to-all-start = ((f32[8,64,288]{2,1,0:T(8,128)}), f32[8,64,288]{2,1,0:T(8,128)S(1)}, u32[]{:S(2)}, u32[]{:S(2)}) async-start(f32[8,64,288]{2,1,0:T(8,128)} %bitcast.7), calls=%async_computation | async-start | bytes 1572864 | tf_op jit(solution)/shard_map/all_to_all | solution.py:21
  651.3 20.6 %all-to-all-start.1 = ((f32[16,4,288]{2,1,0:T(4,128)}), f32[16,4,288]{2,1,0:T(4,128)S(1)}, u32[]{:S(2)}, u32[]{:S(2)}) async-start(f32[16,4,288]{2,1,0:T(4,128)} %reshape.89), calls=%async_computation.1 | async-start | bytes 196608 | tf_op jit(solution)/shard_map/all_to_all | solution.py:21
where the time goes:
time: 684 us; the launch traced here: 679 us
  blocking collectives  311 us (45%)
  matrix products  200 us (29%)
  other arithmetic  82.4 us (12%)
  local copies, waits for them, and re-layouts  51.7 us (8%)
  starting transfers between devices  18.2 us (3%)
  waiting for transfers between devices  15.9 us (2%)
    all_gather x1, blocking collectives, body(): gathered = lax.all_gather(momenta, ('gx', 'gz', 'ta'), axis=0, tiled=True)  311 us
    dot_general x1, matrix products, single_block(): third = jnp.einsum('ms,cs->mc', -sine, summed_part, precision=high)  94.9 us
    dot_general x1, matrix products, single_block(): second = jnp.einsum('ms,cs->mc', cosine, diff_part, precision=high)  80 us
    dot_general x1, other arithmetic, single_block(): first = jnp.einsum('ms,cs->mc', cosine - sine, plain_re, precision=high)  72.3 us
    slice x1, local copies, waits for them, and re-layouts, body(): plain_im = propagator[1].reshape(144, local_sites)  32.7 us
    dot_general x1, matrix products, single_block(): first = jnp.einsum('ms,cs->mc', cosine - sine, plain_re, precision=high)  20.4 us
    all_to_all x2, starting transfers between devices, summed_on_arrival(): lax.all_to_all(in_blocks(array, dim, devices), axis, 0, 0, tiled=True)  18.2 us
    all_to_all x2, waiting for transfers between devices, summed_on_arrival(): lax.all_to_all(in_blocks(array, dim, devices), axis, 0, 0, tiled=True)  15.9 us
  transfers between devices with their start and end apart: 2, of which 2 were waited for; matrix products, arithmetic and copies ran while one was open for 0% of the time, Pallas kernels for 0%

commit v1 on v0

--- a/solution.py
+++ b/solution.py
@@ -130,7 +130,12 @@
     plain_im = propagator[1].reshape(144, local_sites)
     diff_part = plain_im - plain_re
     summed_part = plain_re + plain_im
-    gathered = lax.all_gather(momenta, ("gx", "gz", "ta"), axis=0, tiled=True)
+    gathered = jnp.concatenate(
+        lax.all_to_all(
+            jnp.stack([momenta] * lax.axis_size(("gx", "gz", "ta"))), ("gx", "gz", "ta"), 0, 0
+        ),
+        axis=0,
+    )
     spatial = lax.axis_size("gx") * lax.axis_size("gz")
     ordered = gathered.reshape(spatial, lax.axis_size("ta"), mine, 4)
     ordered = jnp.transpose(ordered, (1, 0, 2, 3)).reshape(-1, 4)

time: 684 us -> 385 us (0.56)
  blocking collectives: 311 us -> 0 us
    all_gather x1 -> x0, blocking collectives: 311 us -> none  [body(): gathered = lax.all_gather(momenta, ('gx', 'gz', 'ta'), axis=0, tiled=True)]
    all_to_all x0 -> x1, starting transfers between devices: none -> 11.5 us  [body(): lax.all_to_all(jnp.stack([momenta] * lax.axis_size(('gx', 'gz', 'ta'))),...]
  transfers between devices with their start and end apart: 2 -> 3, of which waited for: 2 -> 2; matrix products, arithmetic and copies ran while one was open for 0% -> 14% of each run, Pallas kernels for 0% -> 0%
where the time goes in v1:
time: 385 us; the launch traced here: 379 us
  matrix products  200 us (52%)
  other arithmetic  82.3 us (21%)
  local copies, waits for them, and re-layouts  53.1 us (14%)
  starting transfers between devices  24.7 us (6%)
  waiting for transfers between devices  19.1 us (5%)
    dot_general x1, matrix products, single_block(): third = jnp.einsum('ms,cs->mc', -sine, summed_part, precision=high)  94.8 us
    dot_general x1, matrix products, single_block(): second = jnp.einsum('ms,cs->mc', cosine, diff_part, precision=high)  79.9 us
    dot_general x1, other arithmetic, single_block(): first = jnp.einsum('ms,cs->mc', cosine - sine, plain_re, precision=high)  72.2 us
    slice x1, local copies, waits for them, and re-layouts, body(): plain_im = propagator[1].reshape(144, local_sites)  32.7 us
    dot_general x1, matrix products, single_block(): first = jnp.einsum('ms,cs->mc', cosine - sine, plain_re, precision=high)  20.4 us
    all_to_all x2, waiting for transfers between devices, summed_on_arrival(): lax.all_to_all(in_blocks(array, dim, devices), axis, 0, 0, tiled=True)  19.1 us
    all_to_all x2, starting transfers between devices, summed_on_arrival(): lax.all_to_all(in_blocks(array, dim, devices), axis, 0, 0, tiled=True)  13.2 us
    all_to_all x1, starting transfers between devices, body(): lax.all_to_all(jnp.stack([momenta] * lax.axis_size(('gx', 'gz', 'ta'))),...  11.5 us
  transfers between devices with their start and end apart: 3, of which 2 were waited for; matrix products, arithmetic and copies ran while one was open for 14% of the time, Pallas kernels for 0%

profile of v1, /device:TPU:1, one launch (start us, length us, event | category | flops | bytes accessed | tf_op | source)
XLA Modules:
  0.0 379.4 jit_solution(7399322305674453684)
XLA Ops:
  0.0 1.4 stack.8
  1.4 11.5 %all-to-all-start = ((s32[128,4,4]{2,1,0:T(4,128)}), s32[128,4,4]{2,1,0:T(4,128)S(1)}, u32[]{:S(2)}, u32[]{:S(2)}) async-start(s32[128,4,4]{2,1,0:T(4,128)} %stack.8), calls=%async_computation | async-start | bytes 524288 | tf_op jit(solution)/shard_map/all_to_all | solution.py:134
  12.9 32.7 %slice_reduce_fusion = (f32[12,12,8192]{2,1,0:T(8,128)}, f32[12,12,8192]{2,1,0:T(8,128)}) fusion(f32[2,12,12,8192]{3,0,2,1:T(2,128)} %param.5), kind=kLoop, calls=%fused_computation.15 | loop fusion | bytes 18874368 | tf_op jit(solution)/shard_map/slice | solution.py:130
  45.6 6.0 %reshape_squeeze.12 = f32[144,8192]{1,0:T(8,128)} reshape(f32[12,12,8192]{2,1,0:T(8,128)} %get-tuple-element.24) | data formatting | bytes 9437184 | tf_op jit(solution)/shard_map/reshape;squeeze | solution.py:129
  51.6 6.0 %reshape_squeeze.13 = f32[144,8192]{1,0:T(8,128)} reshape(f32[12,12,8192]{2,1,0:T(8,128)} %get-tuple-element.23) | data formatting | bytes 9437184 | tf_op jit(solution)/shard_map/reshape;squeeze | solution.py:130
  57.6 6.9 %fusion.108 = f32[144,8192]{1,0:T(8,128)} fusion(f32[144,8192]{1,0:T(8,128)} %reshape_squeeze.13, f32[144,8192]{1,0:T(8,128)} %reshape_squeeze.12), kind=kLoop, calls=%fused_computation.13.clone.clone.clone.2 | loop fusion | flops 1179648 | bytes 14155776 | tf_op jit(solution)/shard_map/while/body/eval_jaxpr/ms,cs->mc/dot_general | solution.py:112
  64.5 0.0 slice-done
  64.5 1.2 copy-done
  65.7 3.0 fusion.110
  68.7 0.0 all-to-all-done
  68.7 1.0 copy.104
  69.7 0.2 squeeze.19
  70.0 0.0 slice-start.3
  70.0 0.0 slice-start.6
  70.0 72.2 %fusion.106 = f32[512,8192]{1,0:T(8,128)} fusion(s32[8192]{0:T(1024)S(1)} %get-tuple-element.46, s32[512]{0:T(512)S(1)} %bitcast.106, s32[8192]{0:T(1024)S(1)} %get-tuple-element.45, s32[512]{0:T(512)S(1)} %bitcast.109, s32[8192]{0:T(1024)S(1)} %get-tuple-element.42, s32[512]{0:T(512)S(1)} %bitcast.112, s32[8192]{0:T(1024)S(1)} %get-tuple-element.44, ...), kind=kLoop, calls=%fused_computation.9.clone.1 | loop fusion | flops 88080384 | bytes 16916480 | tf_op jit(solution)/shard_map/while/body/eval_jaxpr/ms,cs->mc/dot_general | solution.py:111
  142.2 0.0 slice-done.2
  142.2 0.0 slice-start.7
  142.2 0.0 slice-start.4
  142.2 20.4 %fusion.5 = f32[512,144]{0,1:T(8,128)S(1)} fusion(f32[144,8192]{1,0:T(8,128)S(1)} %bitcast.86, f32[512,8192]{1,0:T(8,128)} %fusion.106), kind=kOutput, calls=%fused_computation.8 | convolution fusion | flops 7247757312 | bytes 21790720 | tf_op jit(solution)/shard_map/while/body/eval_jaxpr/ms,cs->mc/dot_general | solution.py:111
  162.7 0.0 slice-start.5
  162.7 79.9 %fusion.20 = f32[512,144]{0,1:T(8,128)S(1)} fusion(f32[512,144]{0,1:T(8,128)S(1)} %fusion.5, s32[8192]{0:T(1024)S(1)} %get-tuple-element.46, s32[512]{0:T(512)S(1)} %bitcast.107, s32[8192]{0:T(1024)S(1)} %get-tuple-element.45, s32[512]{0:T(512)S(1)} %bitcast.110, s32[8192]{0:T(1024)S(1)} %get-tuple-element.42, s32[512]{0:T(512)S(1)} %bitcast.113, ...), kind=kOutput, calls=%fused_computation.25 | convolution fusion | flops 7331717120 | bytes 5447680 | tf_op jit(solution)/shard_map/while/body/eval_jaxpr/ms,cs->mc/dot_general | solution.py:112
  242.7 0.0 copy-start.1
  242.7 0.0 copy-start.3
  242.7 0.0 copy-start.2
  242.7 94.8 %fusion.25 = f32[512,144]{0,1:T(8,128)S(1)} fusion(f32[512,144]{0,1:T(8,128)S(1)} %fusion.5, s32[8192]{0:T(1024)S(1)} %get-tuple-element.46, s32[512]{0:T(512)S(1)} %bitcast.108, s32[8192]{0:T(1024)S(1)} %get-tuple-element.45, s32[512]{0:T(512)S(1)} %bitcast.111, s32[8192]{0:T(1024)S(1)} %get-tuple-element.42, s32[512]{0:T(512)S(1)} %bitcast.114, ...), kind=kOutput, calls=%fused_computation.26 | convolution fusion | flops 7335911424 | bytes 5447680 | tf_op jit(solution)/shard_map/while/body/eval_jaxpr/ms,cs->mc/dot_general | solution.py:113
  337.6 1.2 copy.78
  338.7 7.1 %all-to-all-start.1 = ((f32[8,64,288]{2,1,0:T(8,128)}), f32[8,64,288]{2,1,0:T(8,128)S(1)}, u32[]{:S(2)}, u32[]{:S(2)}) async-start(f32[8,64,288]{2,1,0:T(8,128)} %bitcast.7), calls=%async_computation.1 | async-start | bytes 1572864 | tf_op jit(solution)/shard_map/all_to_all | solution.py:21
  345.8 0.2 fusion.61
  346.0 13.3 %all-to-all-done.1 = f32[8,64,288]{2,1,0:T(8,128)S(1)} async-done(((f32[8,64,288]{2,1,0:T(8,128)}), f32[8,64,288]{2,1,0:T(8,128)S(1)}, u32[]{:S(2)}, u32[]{:S(2)}) %all-to-all-start.1) | async-done | bytes 589856 | tf_op jit(solution)/shard_map/all_to_all | solution.py:21
  359.4 0.7 reshape.87
  360.1 6.2 %all-to-all-start.2 = ((f32[16,4,288]{2,1,0:T(4,128)}), f32[16,4,288]{2,1,0:T(4,128)S(1)}, u32[]{:S(2)}, u32[]{:S(2)}) async-start(f32[16,4,288]{2,1,0:T(4,128)} %reshape.87), calls=%async_computation.2 | async-start | bytes 196608 | tf_op jit(solution)/shard_map/all_to_all | solution.py:21
  366.2 0.2 fusion.60
  366.4 5.7 %all-to-all-done.2 = f32[16,4,288]{2,1,0:T(4,128)S(1)} async-done(((f32[16,4,288]{2,1,0:T(4,128)}), f32[16,4,288]{2,1,0:T(4,128)S(1)}, u32[]{:S(2)}, u32[]{:S(2)}) %all-to-all-start.2) | async-done | bytes 73760 | tf_op jit(solution)/shard_map/all_to_all | solution.py:21
  372.2 0.1 mul.133
  372.3 0.6 fusion.54
  372.9 0.6 fusion.58
  373.5 0.6 fusion.18
  374.1 0.2 copy.90
  374.3 0.4 copy.91
  374.6 0.5 fusion.46
  375.1 0.6 fusion.19
  375.7 0.2 copy.86
  375.9 0.4 copy.87
  376.2 0.5 fusion.48
  376.7 0.5 fusion.16
  377.2 0.5 fusion.17
  377.6 0.1 pad_maximum_fusion
  377.7 1.5 copy.94
  (27 shorter events, 0.2 us)
Async XLA Ops:
  1.4 67.3 %all-to-all-start = ((s32[128,4,4]{2,1,0:T(4,128)}), s32[128,4,4]{2,1,0:T(4,128)S(1)}, u32[]{:S(2)}, u32[]{:S(2)}) async-start(s32[128,4,4]{2,1,0:T(4,128)} %stack.8), calls=%async_computation | async-start | bytes 524288 | tf_op jit(solution)/shard_map/all_to_all | solution.py:134
  51.6 12.9 %slice-start = ((s8[4718592]{0:T(1024)(128)(4,1)}), s8[524288]{0:T(1024)(128)(4,1)S(1)}, s32[]{:S(2)}) async-start(s8[4718592]{0:T(1024)(128)(4,1)} %bitcast.83), calls=%async_computation.3 | async-start | bytes 1048576
  57.6 6.9 %slice-start.1 = ((s8[4718592]{0:T(1024)(128)(4,1)}), s8[4194304]{0:T(1024)(128)(4,1)S(1)}, s32[]{:S(2)}) async-start(s8[4718592]{0:T(1024)(128)(4,1)} %bitcast.83), calls=%async_computation.4 | async-start | bytes 8388608
  57.6 8.1 %copy-start = (f32[144,8192]{1,0:T(8,128)S(1)}, f32[144,8192]{1,0:T(8,128)}, u32[]{:S(2)}) copy-start(f32[144,8192]{1,0:T(8,128)} %reshape_squeeze.13) | copy-start | bytes 14155780
  65.7 76.5 %slice-start.2 = ((s8[4718592]{0:T(1024)(128)(4,1)}), s8[524288]{0:T(1024)(128)(4,1)S(1)}, s32[]{:S(2)}) async-start(s8[4718592]{0:T(1024)(128)(4,1)} %bitcast.85), calls=%async_computation.5 | async-start | bytes 1048576
  70.0 72.2 %slice-start.3 = ((s8[4718592]{0:T(1024)(128)(4,1)}), s8[4194304]{0:T(1024)(128)(4,1)S(1)}, s32[]{:S(2)}) async-start(s8[4718592]{0:T(1024)(128)(4,1)} %bitcast.85), calls=%async_computation.6 | async-start | bytes 8388608
  70.0 92.7 %slice-start.6 = ((s8[4718592]{0:T(1024)(128)(4,1)}), s8[4194304]{0:T(1024)(128)(4,1)S(1)}, s32[]{:S(2)}) async-start(s8[4718592]{0:T(1024)(128)(4,1)} %bitcast.89), calls=%async_computation.9 | async-start | bytes 8388608
  142.2 20.5 %slice-start.7 = ((s8[4718592]{0:T(1024)(128)(4,1)}), s8[524288]{0:T(1024)(128)(4,1)S(1)}, s32[]{:S(2)}) async-start(s8[4718592]{0:T(1024)(128)(4,1)} %bitcast.89), calls=%async_computation.10 | async-start | bytes 1048576
  142.2 100.4 %slice-start.4 = ((s8[4718592]{0:T(1024)(128)(4,1)}), s8[524288]{0:T(1024)(128)(4,1)S(1)}, s32[]{:S(2)}) async-start(s8[4718592]{0:T(1024)(128)(4,1)} %bitcast.87), calls=%async_computation.7 | async-start | bytes 1048576
  162.7 79.9 %slice-start.5 = ((s8[4718592]{0:T(1024)(128)(4,1)}), s8[4194304]{0:T(1024)(128)(4,1)S(1)}, s32[]{:S(2)}) async-start(s8[4718592]{0:T(1024)(128)(4,1)} %bitcast.87), calls=%async_computation.8 | async-start | bytes 8388608
  242.7 103.1 %copy-start.1 = (s32[16]{0:T(128)S(1)}, s32[16]{0:T(128)}, u32[]{:S(2)}) copy-start(s32[16]{0:T(128)} %param.7) | copy-start | bytes 196
  242.7 103.1 %copy-start.3 = (f32[16,16]{0,1:T(8,128)S(1)}, f32[16,16]{0,1:T(8,128)}, u32[]{:S(2)}) copy-start(f32[16,16]{0,1:T(8,128)} %constant.146) | copy-start | bytes 3076
  242.7 123.5 %copy-start.2 = (f32[16,16]{0,1:T(8,128)S(1)}, f32[16,16]{0,1:T(8,128)}, u32[]{:S(2)}) copy-start(f32[16,16]{0,1:T(8,128)} %constant.147) | copy-start | bytes 3076
  338.7 20.6 %all-to-all-start.1 = ((f32[8,64,288]{2,1,0:T(8,128)}), f32[8,64,288]{2,1,0:T(8,128)S(1)}, u32[]{:S(2)}, u32[]{:S(2)}) async-start(f32[8,64,288]{2,1,0:T(8,128)} %bitcast.7), calls=%async_computation.1 | async-start | bytes 1572864 | tf_op jit(solution)/shard_map/all_to_all | solution.py:21
  360.1 12.1 %all-to-all-start.2 = ((f32[16,4,288]{2,1,0:T(4,128)}), f32[16,4,288]{2,1,0:T(4,128)S(1)}, u32[]{:S(2)}, u32[]{:S(2)}) async-start(f32[16,4,288]{2,1,0:T(4,128)} %reshape.87), calls=%async_computation.2 | async-start | bytes 196608 | tf_op jit(solution)/shard_map/all_to_all | solution.py:21
